TPU v7x, 32 devices: a whole 2x2x4 slice. The times are simulated.
32 devices in a mesh: row: 4 (over z), col: 2 (over y), depth: 4 (over x, core).
Axes of the slice: x: 2, y: 2, z: 4, core: 2. Of those that a mesh axis runs over, the one named last changes fastest.
Arguments:
- factor: float32 [4096, 1536], P(('row', 'col', 'depth')), may hold values from -1 to 4, as said below
- update: float32 [4096, 256], P(('row', 'col', 'depth')), may hold values from -0.375 to 0.375
Outputs:
- new_factor: float32 [4096, 1536], P(('row', 'col', 'depth'))
- new_update: float32 [4096, 256], P(('row', 'col', 'depth'))
Inputs may be any that keep to these rules, and one draw needn't show every extreme that they name: `factor`: zero above the diagonal; each diagonal entry is 1 or more.
All inputs are finite; a program needn't handle non-finite values.
Results may differ from a plain program's by a relative error of at most 0.00013.
Values sent between devices are 32-bit elements; how exact they have to be, the bound alone decides.
A program may use at most 128 MiB of HBM per device.

v0:
```python
import jax
import jax.numpy as jnp
from jax import lax
from jax.sharding import PartitionSpec as P

B = 512
PANELS = 3


def spread(block, axis, owner):
    block = jnp.where(lax.axis_index(axis) == owner, block, jnp.zeros_like(block))
    return lax.psum(block, axis)


def transform(stacked):
    panel_width = stacked.shape[0]
    diag_block = stacked[:, :panel_width]
    v_block = stacked[:, panel_width:]
    update_rank = v_block.shape[1]
    gram_matrix = jnp.dot(stacked, stacked.T, precision=lax.Precision.HIGHEST)
    new_diag = jnp.linalg.cholesky(gram_matrix)
    leading = jax.scipy.linalg.solve_triangular(new_diag, stacked, lower=True)
    coupling = jax.scipy.linalg.solve_triangular(diag_block, v_block, lower=True)
    identity_k = jnp.eye(update_rank, dtype=jnp.float32)
    inner_gram = identity_k + jnp.dot(coupling.T, coupling, precision=lax.Precision.HIGHEST)
    lower_inner = jnp.linalg.cholesky(inner_gram)
    null_basis = jnp.concatenate([-coupling, identity_k], 0)
    second = jax.scipy.linalg.solve_triangular(lower_inner, null_basis.T, lower=True).T
    return jnp.concatenate([leading.T, second], 1)


def on_device(factor, update):
    rows_dev = factor.shape[0]
    row_ids = lax.axis_index(("row", "col", "depth")) * rows_dev + jnp.arange(
        rows_dev, dtype=jnp.int32
    )
    early_slabs = []
    for owner_index in range(PANELS):
        width = (owner_index + 1) * B
        early_slabs.append(
            (
                spread(factor[:, :width], ("row", "col"), owner_index),
                spread(update, ("row", "col"), owner_index),
            )
        )
    for panel_index in range(PANELS):
        panel_start = panel_index * B
        panel_cols = factor[:, panel_start : panel_start + B]
        stacked = jnp.concatenate([panel_cols, update], 1)
        slab_cols, slab_update = early_slabs[panel_index]
        current = jnp.concatenate([slab_cols[:, panel_start : panel_start + B], slab_update], 1)
        diag_rows = lax.all_gather(current, "depth", axis=0, tiled=True)
        rotation = transform(diag_rows)
        for later in range(panel_index + 1, PANELS):
            later_cols, later_update = early_slabs[later]
            joined = jnp.concatenate(
                [later_cols[:, panel_start : panel_start + B], later_update], 1
            )
            early_slabs[later] = (
                later_cols,
                jnp.dot(joined, rotation[:, B:], precision=lax.Precision.HIGHEST),
            )
        moved = jnp.dot(stacked, rotation, precision=lax.Precision.HIGHEST)
        col_ids = panel_start + jnp.arange(B, dtype=jnp.int32)
        new_cols = jnp.where(row_ids[:, None] >= col_ids[None, :], moved[:, :B], jnp.float32(0.0))
        update = jnp.where(row_ids[:, None] >= panel_start, moved[:, B:], update)
        factor = factor.at[:, panel_start : panel_start + B].set(new_cols)
    return (factor, update)


def solution(mesh):
    return jax.shard_map(
        on_device,
        mesh=mesh,
        in_specs=(P(("row", "col", "depth"), None), P(("row", "col", "depth"), None)),
        out_specs=(P(("row", "col", "depth"), None), P(("row", "col", "depth"), None)),
        check_vma=False,
    )
```

profile of v0, /device:TPU:0, one launch (start us, length us, event | category | flops | bytes accessed | tf_op | source)
XLA Modules:
  0.0 1116.5 jit_solution(5682356321159899076)
XLA Ops:
  11.8 103.0 %all-reduce.5.cloned.1.call-done = (f32[128,256]{1,0:T(8,128)}, f32[128,512]{1,0:T(8,128)}, f32[128,256]{1,0:T(8,128)}, f32[128,1024]{1,0:T(8,128)}, f32[128,256]{1,0:T(8,128)}, /*index=5*/f32[128,1536]{1,0:T(8,128)}) async-done(((f32[128,256]{1,0:T(8,128)}, f32[128,512]{1,0:T(8,128)}, f32[128,256]{1,0:T(8,128)}, f32[128,1024]{1,0:T(8,128)}, f32[128,256]{1,0:T(8,128)}, /*index=5*/f32[128,1536]{1,0:T(8,128)}), ...) | async-done | bytes 1966096 | tf_op jit(solution)/shard_map/psum | solution.py:12
  122.2 13.5 %all-gather.4.cloned.1.call-done = f32[512,768]{1,0:T(8,128)} async-done(((f32[128,768]{1,0:T(8,128)}), f32[512,768]{1,0:T(8,128)}) %all-gather.4.cloned.1.call-update) | async-done | bytes 1572880 | tf_op jit(solution)/shard_map/all_gather | solution.py:52
  149.8 39.5 %custom-call.57 = f32[4,128,128]{1,2,0:T(8,128)S(1)} custom-call(f32[4,128,128]{2,1,0:T(8,128)S(1)} %get-tuple-element.105), custom_call_target="InvertDiagBlocksLowerTriangular" | custom-call | tf_op jit(solution)/shard_map/jit(_solve_triangular)/triangular_solve | solution.py:23
  224.6 12.1 %cholesky.570 = f32[128,128]{1,0:T(8,128)S(1)} custom-call(f32[128,128]{1,0:T(8,128)S(1)} %convolution_subtract_fusion.29), custom_call_target="Cholesky" | custom-call | tf_op jit(solution)/shard_map/jit(cholesky)/cholesky | solution.py:26
  247.1 19.7 %custom-call.59 = f32[2,128,128]{1,2,0:T(8,128)S(1)} custom-call(f32[2,128,128]{2,1,0:T(8,128)S(1)} %get-tuple-element.106), custom_call_target="InvertDiagBlocksLowerTriangular" | custom-call | tf_op jit(solution)/shard_map/jit(_solve_triangular)/triangular_solve | solution.py:28
  280.0 13.2 %cholesky.492 = f32[128,128]{1,0:T(8,128)} custom-call(f32[128,128]{1,0:T(8,128)} %cholesky.773), custom_call_target="Cholesky" | custom-call | tf_op jit(solution)/shard_map/jit(cholesky)/cholesky | solution.py:21
  313.0 13.3 %cholesky.511 = f32[128,128]{1,0:T(8,128)} custom-call(f32[128,128]{1,0:T(8,128)} %cholesky.777), custom_call_target="Cholesky" | custom-call | tf_op jit(solution)/shard_map/jit(cholesky)/cholesky | solution.py:21
  344.2 13.2 %cholesky.532 = f32[128,128]{1,0:T(8,128)} custom-call(f32[128,128]{1,0:T(8,128)} %cholesky.782), custom_call_target="Cholesky" | custom-call | tf_op jit(solution)/shard_map/jit(cholesky)/cholesky | solution.py:21
  374.6 13.2 %cholesky.545 = f32[128,128]{1,0:T(8,128)} custom-call(f32[128,128]{1,0:T(8,128)} %convolution_subtract_fusion.32), custom_call_target="Cholesky" | custom-call | tf_op jit(solution)/shard_map/jit(cholesky)/cholesky | solution.py:21
  398.1 13.6 %while.21 = (s32[]{:T(128)}, f32[512,512]{1,0:T(8,128)}, s32[4,2]{0,1:T(2,128)S(1)}, f32[4,128,128]{2,1,0:T(8,128)}, s32[]{:T(128)}) while((s32[]{:T(128)}, f32[512,512]{1,0:T(8,128)}, s32[4,2]{0,1:T(2,128)S(1)}, f32[4,128,128]{2,1,0:T(8,128)}, s32[]{:T(128)}) %tuple.230), condition=%wide.while_cond.3, body=%wide.while_body.3.sunk | while | flops 2 | bytes 132205 | solution.py:22
  411.7 40.7 %custom-call.56 = f32[4,128,128]{1,2,0:T(8,128)} custom-call(f32[4,128,128]{2,1,0:T(8,128)} %get-tuple-element.104), custom_call_target="InvertDiagBlocksLowerTriangular" | custom-call | tf_op jit(solution)/shard_map/jit(_solve_triangular)/triangular_solve | solution.py:22
  490.0 39.5 %custom-call.64 = f32[4,128,128]{1,2,0:T(8,128)S(1)} custom-call(f32[4,128,128]{2,1,0:T(8,128)S(1)} %get-tuple-element.108), custom_call_target="InvertDiagBlocksLowerTriangular" | custom-call | tf_op jit(solution)/shard_map/jit(_solve_triangular)/triangular_solve | solution.py:23
  563.9 12.1 %cholesky.665 = f32[128,128]{1,0:T(8,128)S(1)} custom-call(f32[128,128]{1,0:T(8,128)S(1)} %convolution_subtract_fusion.28), custom_call_target="Cholesky" | custom-call | tf_op jit(solution)/shard_map/jit(cholesky)/cholesky | solution.py:26
  585.5 20.3 %custom-call.66 = f32[2,128,128]{1,2,0:T(8,128)} custom-call(f32[2,128,128]{2,1,0:T(8,128)S(1)} %get-tuple-element.109), custom_call_target="InvertDiagBlocksLowerTriangular" | custom-call | tf_op jit(solution)/shard_map/jit(_solve_triangular)/triangular_solve | solution.py:28
  641.3 11.9 %cholesky.606 = f32[128,128]{1,0:T(8,128)S(1)} custom-call(f32[128,128]{1,0:T(8,128)S(1)} %cholesky.793), custom_call_target="Cholesky" | custom-call | tf_op jit(solution)/shard_map/jit(cholesky)/cholesky | solution.py:21
  666.6 13.2 %cholesky.627 = f32[128,128]{1,0:T(8,128)} custom-call(f32[128,128]{1,0:T(8,128)} %cholesky.798), custom_call_target="Cholesky" | custom-call | tf_op jit(solution)/shard_map/jit(cholesky)/cholesky | solution.py:21
  727.1 40.3 %custom-call.63 = f32[4,128,128]{1,2,0:T(8,128)} custom-call(f32[4,128,128]{2,1,0:T(8,128)S(1)} %get-tuple-element.107), custom_call_target="InvertDiagBlocksLowerTriangular" | custom-call | tf_op jit(solution)/shard_map/jit(_solve_triangular)/triangular_solve | solution.py:22
  803.4 40.9 %custom-call.71 = f32[4,128,128]{1,2,0:T(8,128)} custom-call(f32[4,128,128]{2,1,0:T(8,128)} %get-tuple-element.111), custom_call_target="InvertDiagBlocksLowerTriangular" | custom-call | tf_op jit(solution)/shard_map/jit(_solve_triangular)/triangular_solve | solution.py:23
  879.9 13.6 %cholesky.760 = f32[128,128]{1,0:T(8,128)} custom-call(f32[128,128]{1,0:T(8,128)} %convolution_subtract_fusion.27), custom_call_target="Cholesky" | custom-call | tf_op jit(solution)/shard_map/jit(cholesky)/cholesky | solution.py:26
  905.1 21.1 %custom-call.73 = f32[2,128,128]{1,2,0:T(8,128)} custom-call(f32[2,128,128]{2,1,0:T(8,128)} %get-tuple-element.112), custom_call_target="InvertDiagBlocksLowerTriangular" | custom-call | tf_op jit(solution)/shard_map/jit(_solve_triangular)/triangular_solve | solution.py:28
  965.4 13.3 %cholesky.701 = f32[128,128]{1,0:T(8,128)} custom-call(f32[128,128]{1,0:T(8,128)} %cholesky.809), custom_call_target="Cholesky" | custom-call | tf_op jit(solution)/shard_map/jit(cholesky)/cholesky | solution.py:21
  995.8 13.2 %cholesky.722 = f32[128,128]{1,0:T(8,128)} custom-call(f32[128,128]{1,0:T(8,128)} %cholesky.814), custom_call_target="Cholesky" | custom-call | tf_op jit(solution)/shard_map/jit(cholesky)/cholesky | solution.py:21
  1025.4 13.2 %cholesky.735 = f32[128,128]{1,0:T(8,128)} custom-call(f32[128,128]{1,0:T(8,128)} %convolution_subtract_fusion.30), custom_call_target="Cholesky" | custom-call | tf_op jit(solution)/shard_map/jit(cholesky)/cholesky | solution.py:21
  1058.7 39.6 %custom-call.70 = f32[4,128,128]{1,2,0:T(8,128)S(1)} custom-call(f32[4,128,128]{2,1,0:T(8,128)S(1)} %get-tuple-element.110), custom_call_target="InvertDiagBlocksLowerTriangular" | custom-call | tf_op jit(solution)/shard_map/jit(_solve_triangular)/triangular_solve | solution.py:22
  (433 shorter events, 590.4 us)
Async XLA Ops:
  7.2 107.7 %all-reduce.5.cloned.1.call-start = ((), (), s32[]{:S(2)}) async-start(), calls=%async_computation.3 | async-start | bytes 3932160 | tf_op jit(solution)/shard_map/psum | solution.py:12
  8.3 2.6 copy-start.13
  11.8 124.0 %all-gather.4.cloned.1.call-start = ((), (), s32[]{:S(2)}) async-start(), calls=%async_computation | async-start | bytes 1966080 | tf_op jit(solution)/shard_map/all_gather | solution.py:52
  114.9 5.6 copy-start.32
  114.9 6.5 copy-start.25
  116.8 359.1 %all-gather.6.cloned.1.call-start = ((), (), s32[]{:S(2)}) async-start(), calls=%async_computation.1 | async-start | bytes 1966080 | tf_op jit(solution)/shard_map/all_gather | solution.py:52
  117.0 419.1 %copy-start.6 = (f32[256,256]{1,0:T(8,128)}, f32[256,256]{1,0:T(8,128)S(1)}, u32[]{:S(2)}) copy-start(f32[256,256]{1,0:T(8,128)S(1)} %copy.9) | copy-start | bytes 786436
  135.8 53.6 %copy-start = (f32[512,768]{1,0:T(8,128)S(1)}, f32[512,768]{1,0:T(8,128)}, u32[]{:S(2)}) copy-start(f32[512,768]{1,0:T(8,128)} %all-gather.4.cloned.1.call-done) | copy-start | bytes 4718596
  196.0 44.9 %copy-start.46 = (s32[2]{0:T(128)S(1)}, s32[2]{0:T(128)}, u32[]{:S(2)}) copy-start(s32[2]{0:T(128)} %iota_multiply_fusion) | copy-start | bytes 28
  456.1 334.2 %all-gather.8.cloned.1.call-start = ((), (), s32[]{:S(2)}) async-start(), calls=%async_computation.2 | async-start | bytes 1966080 | tf_op jit(solution)/shard_map/all_gather | solution.py:52
  465.2 4.0 copy-start.21
  465.2 4.0 copy-start.38
  467.8 3.1 copy-start.44
  475.9 53.6 %copy-start.1 = (f32[512,768]{1,0:T(8,128)S(1)}, f32[512,768]{1,0:T(8,128)}, u32[]{:S(2)}) copy-start(f32[512,768]{1,0:T(8,128)} %all-gather.6.cloned.1.call-done) | copy-start | bytes 4718596
  605.8 2.3 copy-start.40
  714.5 53.0 %copy-start.29 = (f32[128,256]{1,0:T(8,128)S(1)}, f32[128,256]{1,0:T(8,128)}, u32[]{:S(2)}) copy-start(f32[128,256]{1,0:T(8,128)} %fusion.47) | copy-start | bytes 393220
  715.6 54.1 %copy-start.19 = (f32[128,512]{1,0:T(8,128)S(1)}, f32[128,512]{1,0:T(8,128)}, u32[]{:S(2)}) copy-start(f32[128,512]{1,0:T(8,128)} %get-tuple-element.209) | copy-start | bytes 786436
  767.5 4.4 copy-start.5
  767.5 4.4 copy-start.8
  779.3 4.1 copy-start.43
  790.3 54.0 %copy-start.2 = (f32[512,768]{1,0:T(8,128)S(1)}, f32[512,768]{1,0:T(8,128)}, u32[]{:S(2)}) copy-start(f32[512,768]{1,0:T(8,128)} %all-gather.8.cloned.1.call-done) | copy-start | bytes 4718596
  844.3 2.9 copy-start.33
  926.2 2.2 copy-start.41
  1106.2 2.6 copy-start.42
  (27 other events, 26.4 us)
Sparse Core Ops, SparseCore 0:
  12.9 101.9 all-reduce.4
  117.0 18.7 all-gather.3
  456.2 19.6 all-gather.5
  770.6 19.6 all-gather.7
where the time goes:
time: 1120 us
  other arithmetic  731 us (65%)
  waiting for transfers between devices  128 us (11%)
  local copies, waits for them, and re-layouts  125 us (11%)
  matrix products  105 us (9%)
  between operations  26.8 us (2%)
    another operation x44, other arithmetic, transform(): new_diag = jnp.linalg.cholesky(gram_matrix)  280 us
    another operation x6, other arithmetic, transform(): jax.scipy.linalg.solve_triangular(diag_block, v_block, lower=True)  126 us
    another operation x7, other arithmetic, transform(): leading = jax.scipy.linalg.solve_triangular(new_diag, stacked, lower=True)  125 us
    another operation x20, other arithmetic, transform(): lower_inner = jnp.linalg.cholesky(inner_gram)  111 us
    psum x1, waiting for transfers between devices, spread(): return lax.psum(block, axis)  103 us
    another operation x7, other arithmetic, transform(): jax.scipy.linalg.solve_triangular(lower_inner, null_basis.T, lower=True)  65.2 us
    another operation x43, local copies, waits for them, and re-layouts, transform(): leading = jax.scipy.linalg.solve_triangular(new_diag, stacked, lower=True)  38.1 us
    another operation x36, local copies, waits for them, and re-layouts, transform(): jax.scipy.linalg.solve_triangular(diag_block, v_block, lower=True)  33.9 us
  transfers between devices with their start and end apart: 4, of which 4 were waited for; matrix products, arithmetic and copies ran while one was open for 3% of the time, Pallas kernels for 0%

commit v1 on v0

--- a/solution.py
+++ b/solution.py
@@ -9,7 +9,7 @@
 
 def spread(block, axis, owner):
     block = jnp.where(lax.axis_index(axis) == owner, block, jnp.zeros_like(block))
-    return lax.psum(block, axis)
+    return jnp.sum(lax.all_gather(block, axis), axis=0)
 
 
 def transform(stacked):

time: 1120 us -> 1180 us (1.054)
  waiting for transfers between devices: 128 us -> 207 us
  other arithmetic: 731 us -> 713 us
    all_gather x0 -> x6, waiting for transfers between devices: none -> 164 us  [spread(): return jnp.sum(lax.all_gather(block, axis), axis=0)]
    psum x1 -> x0, waiting for transfers between devices: 103 us -> none  [spread(): return lax.psum(block, axis)]
    another operation x44, other arithmetic: 280 us -> 252 us  [transform(): new_diag = jnp.linalg.cholesky(gram_matrix)]
    all_gather x3, waiting for transfers between devices: 24.8 us -> 42.1 us  [on_device(): diag_rows = lax.all_gather(current, 'depth', axis=0, tiled=True)]
    reduce_sum x0 -> x6, other arithmetic: none -> 13.2 us  [spread(): return jnp.sum(lax.all_gather(block, axis), axis=0)]
  transfers between devices with their start and end apart: 4 -> 9, of which waited for: 4 -> 7; matrix products, arithmetic and copies ran while one was open for 3% -> 51% of each run, Pallas kernels for 0% -> 0%
where the time goes in v1:
time: 1180 us; the launch traced here: 1170 us
  other arithmetic  713 us (60%)
  waiting for transfers between devices  207 us (18%)
  local copies, waits for them, and re-layouts  119 us (10%)
  matrix products  99.7 us (8%)
  between operations  27 us (2%)
    another operation x44, other arithmetic, transform(): new_diag = jnp.linalg.cholesky(gram_matrix)  252 us
    all_gather x6, waiting for transfers between devices, spread(): return jnp.sum(lax.all_gather(block, axis), axis=0)  164 us
    another operation x6, other arithmetic, transform(): jax.scipy.linalg.solve_triangular(diag_block, v_block, lower=True)  125 us
    another operation x7, other arithmetic, transform(): leading = jax.scipy.linalg.solve_triangular(new_diag, stacked, lower=True)  125 us
    another operation x20, other arithmetic, transform(): lower_inner = jnp.linalg.cholesky(inner_gram)  113 us
    another operation x7, other arithmetic, transform(): jax.scipy.linalg.solve_triangular(lower_inner, null_basis.T, lower=True)  64.5 us
    all_gather x3, waiting for transfers between devices, on_device(): diag_rows = lax.all_gather(current, 'depth', axis=0, tiled=True)  42.1 us
    another operation x43, local copies, waits for them, and re-layouts, transform(): leading = jax.scipy.linalg.solve_triangular(new_diag, stacked, lower=True)  38.9 us
  transfers between devices with their start and end apart: 9, of which 7 were waited for; matrix products, arithmetic and copies ran while one was open for 51% of the time, Pallas kernels for 0%

profile of v1, /device:TPU:0, one launch (start us, length us, event | category | flops | bytes accessed | tf_op | source)
XLA Modules:
  0.0 1165.5 jit_solution(6988690271727824718)
XLA Ops:
  10.1 43.7 %all-gather.24.cloned.1.call-done = f32[1024,256]{1,0:T(8,128)} async-done(((f32[128,256]{1,0:T(8,128)}), f32[1024,256]{1,0:T(8,128)}) %all-gather.24.cloned.1.call-update) | async-done | bytes 1048592 | tf_op jit(solution)/shard_map/all_gather | solution.py:12
  55.0 49.2 %all-gather.22.cloned.1.call-done = f32[1024,512]{1,0:T(8,128)} async-done(((f32[128,512]{1,0:T(8,128)}), f32[1024,512]{1,0:T(8,128)}) %all-gather.22.cloned.1.call-update) | async-done | bytes 2097168 | tf_op jit(solution)/shard_map/all_gather | solution.py:12
  109.3 15.9 %all-gather.16.cloned.1.call-done = f32[512,768]{1,0:T(8,128)} async-done(((f32[128,768]{1,0:T(8,128)}), f32[512,768]{1,0:T(8,128)}) %all-gather.16.cloned.1.call-update) | async-done | bytes 1572880 | tf_op jit(solution)/shard_map/all_gather | solution.py:52
  202.5 11.9 %cholesky.545 = f32[128,128]{1,0:T(8,128)S(1)} custom-call(f32[128,128]{1,0:T(8,128)S(1)} %convolution_subtract_fusion.32), custom_call_target="Cholesky" | custom-call | tf_op jit(solution)/shard_map/jit(cholesky)/cholesky | solution.py:21
  219.9 13.6 %while.21 = (s32[]{:T(128)}, f32[512,512]{1,0:T(8,128)}, s32[4,2]{0,1:T(2,128)S(1)}, f32[4,128,128]{2,1,0:T(8,128)}, s32[]{:T(128)}) while((s32[]{:T(128)}, f32[512,512]{1,0:T(8,128)}, s32[4,2]{0,1:T(2,128)S(1)}, f32[4,128,128]{2,1,0:T(8,128)}, s32[]{:T(128)}) %tuple.201), condition=%wide.while_cond.3, body=%wide.while_body.3.sunk | while | flops 2 | bytes 132705 | solution.py:22
  244.6 40.7 %custom-call.56 = f32[4,128,128]{1,2,0:T(8,128)} custom-call(f32[4,128,128]{2,1,0:T(8,128)} %get-tuple-element.104), custom_call_target="InvertDiagBlocksLowerTriangular" | custom-call | tf_op jit(solution)/shard_map/jit(_solve_triangular)/triangular_solve | solution.py:22
  285.3 41.1 %custom-call.57 = f32[4,128,128]{1,2,0:T(8,128)} custom-call(f32[4,128,128]{2,1,0:T(8,128)} %get-tuple-element.105), custom_call_target="InvertDiagBlocksLowerTriangular" | custom-call | tf_op jit(solution)/shard_map/jit(_solve_triangular)/triangular_solve | solution.py:23
  356.2 11.9 %cholesky.570 = f32[128,128]{1,0:T(8,128)S(1)} custom-call(f32[128,128]{1,0:T(8,128)S(1)} %convolution_subtract_fusion.29), custom_call_target="Cholesky" | custom-call | tf_op jit(solution)/shard_map/jit(cholesky)/cholesky | solution.py:26
  374.9 20.3 %custom-call.59 = f32[2,128,128]{1,2,0:T(8,128)} custom-call(f32[2,128,128]{2,1,0:T(8,128)S(1)} %get-tuple-element.106), custom_call_target="InvertDiagBlocksLowerTriangular" | custom-call | tf_op jit(solution)/shard_map/jit(_solve_triangular)/triangular_solve | solution.py:28
  413.4 37.1 %all-gather.28.cloned.1.call-done = f32[1024,256]{1,0:T(8,128)} async-done(((f32[128,256]{1,0:T(8,128)}), f32[1024,256]{1,0:T(8,128)}) %all-gather.28.cloned.1.call-update) | async-done | bytes 1048592 | tf_op jit(solution)/shard_map/all_gather | solution.py:12
  458.3 33.8 %all-gather.32.cloned.1.call-done = f32[1024,256]{1,0:T(8,128)} async-done(((f32[128,256]{1,0:T(8,128)}), f32[1024,256]{1,0:T(8,128)}) %all-gather.32.cloned.1.call-update) | async-done | bytes 1048592 | tf_op jit(solution)/shard_map/all_gather | solution.py:12
  494.1 18.0 %all-gather.18.cloned.1.call-done = f32[512,768]{1,0:T(8,128)} async-done(((f32[128,768]{1,0:T(8,128)}), f32[512,768]{1,0:T(8,128)}) %all-gather.18.cloned.1.call-update) | async-done | bytes 1572880 | tf_op jit(solution)/shard_map/all_gather | solution.py:52
  595.8 11.9 %cholesky.640 = f32[128,128]{1,0:T(8,128)S(1)} custom-call(f32[128,128]{1,0:T(8,128)S(1)} %convolution_subtract_fusion.31), custom_call_target="Cholesky" | custom-call | tf_op jit(solution)/shard_map/jit(cholesky)/cholesky | solution.py:21
  627.7 39.9 %custom-call.63 = f32[4,128,128]{1,2,0:T(8,128)} custom-call(f32[4,128,128]{2,1,0:T(8,128)S(1)} %get-tuple-element.107), custom_call_target="InvertDiagBlocksLowerTriangular" | custom-call | tf_op jit(solution)/shard_map/jit(_solve_triangular)/triangular_solve | solution.py:22
  681.2 40.5 %custom-call.64 = f32[4,128,128]{1,2,0:T(8,128)S(1)} custom-call(f32[4,128,128]{2,1,0:T(8,128)} %copy-done.39), custom_call_target="InvertDiagBlocksLowerTriangular" | custom-call | tf_op jit(solution)/shard_map/jit(_solve_triangular)/triangular_solve | solution.py:23
  786.2 20.4 %custom-call.66 = f32[2,128,128]{1,2,0:T(8,128)} custom-call(f32[2,128,128]{2,1,0:T(8,128)S(1)} %get-tuple-element.109), custom_call_target="InvertDiagBlocksLowerTriangular" | custom-call | tf_op jit(solution)/shard_map/jit(_solve_triangular)/triangular_solve | solution.py:28
  853.3 41.1 %custom-call.71 = f32[4,128,128]{1,2,0:T(8,128)} custom-call(f32[4,128,128]{2,1,0:T(8,128)} %get-tuple-element.111), custom_call_target="InvertDiagBlocksLowerTriangular" | custom-call | tf_op jit(solution)/shard_map/jit(_solve_triangular)/triangular_solve | solution.py:23
  936.6 13.2 %cholesky.701 = f32[128,128]{1,0:T(8,128)} custom-call(f32[128,128]{1,0:T(8,128)} %cholesky.809), custom_call_target="Cholesky" | custom-call | tf_op jit(solution)/shard_map/jit(cholesky)/cholesky | solution.py:21
  967.7 13.2 %cholesky.722 = f32[128,128]{1,0:T(8,128)} custom-call(f32[128,128]{1,0:T(8,128)} %cholesky.814), custom_call_target="Cholesky" | custom-call | tf_op jit(solution)/shard_map/jit(cholesky)/cholesky | solution.py:21
  997.4 13.2 %cholesky.735 = f32[128,128]{1,0:T(8,128)} custom-call(f32[128,128]{1,0:T(8,128)} %convolution_subtract_fusion.30), custom_call_target="Cholesky" | custom-call | tf_op jit(solution)/shard_map/jit(cholesky)/cholesky | solution.py:21
  1027.4 39.7 %custom-call.70 = f32[4,128,128]{1,2,0:T(8,128)S(1)} custom-call(f32[4,128,128]{2,1,0:T(8,128)S(1)} %get-tuple-element.110), custom_call_target="InvertDiagBlocksLowerTriangular" | custom-call | tf_op jit(solution)/shard_map/jit(_solve_triangular)/triangular_solve | solution.py:22
  1075.7 13.2 %cholesky.750 = f32[128,128]{1,0:T(8,128)} custom-call(f32[128,128]{1,0:T(8,128)} %cholesky.818), custom_call_target="Cholesky" | custom-call | tf_op jit(solution)/shard_map/jit(cholesky)/cholesky | solution.py:26
  1105.3 13.3 %cholesky.760 = f32[128,128]{1,0:T(8,128)} custom-call(f32[128,128]{1,0:T(8,128)} %convolution_subtract_fusion.27), custom_call_target="Cholesky" | custom-call | tf_op jit(solution)/shard_map/jit(cholesky)/cholesky | solution.py:26
  1130.6 21.1 %custom-call.73 = f32[2,128,128]{1,2,0:T(8,128)} custom-call(f32[2,128,128]{2,1,0:T(8,128)} %get-tuple-element.112), custom_call_target="InvertDiagBlocksLowerTriangular" | custom-call | tf_op jit(solution)/shard_map/jit(_solve_triangular)/triangular_solve | solution.py:28
  (455 shorter events, 607.1 us)
Async XLA Ops:
  7.2 46.5 %all-gather.24.cloned.1.call-start = ((), (), s32[]{:S(2)}) async-start(), calls=%async_computation.4 | async-start | bytes 1179648 | tf_op jit(solution)/shard_map/all_gather | solution.py:12
  9.1 95.2 %all-gather.22.cloned.1.call-start = ((), (), s32[]{:S(2)}) async-start(), calls=%async_computation.3 | async-start | bytes 2359296 | tf_op jit(solution)/shard_map/all_gather | solution.py:12
  10.0 115.2 %all-gather.16.cloned.1.call-start = ((), (), s32[]{:S(2)}) async-start(), calls=%async_computation | async-start | bytes 1966080 | tf_op jit(solution)/shard_map/all_gather | solution.py:52
  106.9 303.9 %all-gather.26.cloned.1.call-start = ((), (), s32[]{:S(2)}) async-start(), calls=%async_computation.5 | async-start | bytes 4718592 | tf_op jit(solution)/shard_map/all_gather | solution.py:12
  107.8 342.8 %all-gather.28.cloned.1.call-start = ((), (), s32[]{:S(2)}) async-start(), calls=%async_computation.6 | async-start | bytes 1179648 | tf_op jit(solution)/shard_map/all_gather | solution.py:12
  218.1 15.4 %copy-start.1 = (f32[512,768]{1,0:T(8,128)S(1)}, f32[512,768]{1,0:T(8,128)}, u32[]{:S(2)}) copy-start(f32[512,768]{1,0:T(8,128)} %all-gather.16.cloned.1.call-done) | copy-start | bytes 4718596
  326.4 3.0 copy-start.35
  332.3 11.8 %copy-start.27 = (f32[256,256]{1,0:T(8,128)}, f32[256,256]{1,0:T(8,128)S(1)}, u32[]{:S(2)}) copy-start(f32[256,256]{1,0:T(8,128)S(1)} %fusion.117) | copy-start | bytes 786436
  332.3 62.8 %copy-start.15 = (f32[128,256]{1,0:T(8,128)S(1)}, f32[128,256]{1,0:T(8,128)}, u32[]{:S(2)}) copy-start(f32[128,256]{1,0:T(8,128)} %copy-done.14) | copy-start | bytes 393220
  332.3 62.8 %copy-start.21 = (f32[128,256]{1,0:T(8,128)S(1)}, f32[128,256]{1,0:T(8,128)}, u32[]{:S(2)}) copy-start(f32[128,256]{1,0:T(8,128)} %copy-done.20) | copy-start | bytes 393220
  353.9 42.2 %copy-start.6 = (f32[256,256]{1,0:T(8,128)S(1)}, f32[256,256]{1,0:T(8,128)}, u32[]{:S(2)}) copy-start(f32[256,256]{1,0:T(8,128)} %copy.9) | copy-start | bytes 786436
  398.9 52.9 %copy-start.4 = (f32[128,768]{1,0:T(8,128)}, f32[128,768]{1,0:T(8,128)S(1)}, u32[]{:S(2)}) copy-start(f32[128,768]{1,0:T(8,128)S(1)} %fusion.179) | copy-start | bytes 1179652
  410.1 82.0 %all-gather.32.cloned.1.call-start = ((), (), s32[]{:S(2)}) async-start(), calls=%async_computation.8 | async-start | bytes 1179648 | tf_op jit(solution)/shard_map/all_gather | solution.py:12
  410.7 101.4 %all-gather.18.cloned.1.call-start = ((), (), s32[]{:S(2)}) async-start(), calls=%async_computation.1 | async-start | bytes 1966080 | tf_op jit(solution)/shard_map/all_gather | solution.py:52
  453.6 358.9 %all-gather.30.cloned.1.call-start = ((), (), s32[]{:S(2)}) async-start(), calls=%async_computation.7 | async-start | bytes 7077888 | tf_op jit(solution)/shard_map/all_gather | solution.py:12
  454.7 385.9 %all-gather.20.cloned.1.call-start = ((), (), s32[]{:S(2)}) async-start(), calls=%async_computation.2 | async-start | bytes 1966080 | tf_op jit(solution)/shard_map/all_gather | solution.py:52
  613.5 54.1 %copy-start = (f32[512,768]{1,0:T(8,128)S(1)}, f32[512,768]{1,0:T(8,128)}, u32[]{:S(2)}) copy-start(f32[512,768]{1,0:T(8,128)} %all-gather.18.cloned.1.call-done) | copy-start | bytes 4718596
  828.1 4.1 copy-start.46
  840.6 53.8 %copy-start.2 = (f32[512,768]{1,0:T(8,128)S(1)}, f32[512,768]{1,0:T(8,128)}, u32[]{:S(2)}) copy-start(f32[512,768]{1,0:T(8,128)} %all-gather.20.cloned.1.call-done) | copy-start | bytes 4718596
  894.4 2.9 copy-start.37
  1075.0 13.8 %copy-start.29 = (f32[256,256]{1,0:T(8,128)}, f32[256,256]{1,0:T(8,128)S(1)}, u32[]{:S(2)}) copy-start(f32[256,256]{1,0:T(8,128)S(1)} %fusion.115) | copy-start | bytes 786436
  1075.0 76.6 %copy-start.7 = (f32[256,256]{1,0:T(8,128)S(1)}, f32[256,256]{1,0:T(8,128)}, u32[]{:S(2)}) copy-start(f32[256,256]{1,0:T(8,128)} %copy.9) | copy-start | bytes 786436
  1075.0 76.6 %copy-start.13 = (f32[512,256]{1,0:T(8,128)S(1)}, f32[512,256]{1,0:T(8,128)}, u32[]{:S(2)}) copy-start(f32[512,256]{1,0:T(8,128)} %fusion.95) | copy-start | bytes 1572868
  1119.5 2.7 copy-start.25
  (33 other events, 36.1 us)
Sparse Core Ops, SparseCore 0:
  10.7 42.9 all-gather.23
  56.4 47.7 all-gather.21
  107.0 18.1 all-gather.15
  127.7 73.0 all-gather.25
  410.2 40.2 all-gather.27
  453.1 38.9 all-gather.31
  493.7 18.3 all-gather.17
  514.8 98.9 all-gather.29
  820.9 19.6 all-gather.19
